TPU v7x, 32 devices: a whole 2x2x4 slice. The times are simulated.
32 devices in a mesh: days: 4 (over y, x), space: 8 (over z, core).
Axes of the slice: x: 2, y: 2, z: 4, core: 2. Of those that a mesh axis runs over, the one named last changes fastest.
Arguments:
- fields: bfloat16 [640, 32, 1440], P('days', 'space')
- month_label: int32 [640], P('days'), may hold values from 0 to 11, as said below
- row_index: int32 [32], P('space'), may hold values from 0 to 31
- area_table: float32 [32], replicated, may hold values from 0.05 to 1
- basis: bfloat16 [64, 32, 1440], P(None, 'space'), may hold values from -6 to 6
Outputs:
- eofs: float32 [64, 32, 1440], P(None, 'space')
- pcs: float32 [640, 64], P('days')
Inputs may be any that keep to these rules, and one draw needn't show every extreme that they name: `month_label`: each day's label differs from floor(12 * day / 640) by at most one; the first day with a given value of floor(12 * day / 640) carries exactly that value; every month labels at least one day.
All inputs are finite; a program needn't handle non-finite values.
Results may differ from a plain program's by a relative error of at most 0.0003.
Values sent between devices are 32-bit elements; how exact they have to be, the bound alone decides.
A program may use at most 64 MiB of HBM per device.

v0:
```python
import jax
import jax.numpy as jnp
from jax import lax
from jax.sharding import PartitionSpec as P

ITERS = 2
HIGH = lax.Precision.HIGHEST


def solve_lower(lower, cover):
    shape = cover.shape
    solved = lax.linalg.triangular_solve(
        lower, cover.reshape(shape[0], -1), left_side=True, lower=True
    )
    return solved.reshape(shape)


def self_gram(cover):
    return jnp.einsum("klc,jlc->kj", cover, cover, precision=HIGH)


def local(fields, month_label, row_index, area_table, basis):
    months = jnp.arange(12, dtype=jnp.int32)
    onehot = (month_label[None, :] == months[:, None]).astype(jnp.bfloat16)
    sums = jnp.einsum("md,dlc->mlc", onehot, fields, preferred_element_type=jnp.float32)
    counts = jnp.sum(onehot.astype(jnp.float32), axis=1)
    sums, counts = lax.psum((sums, counts), "days")
    climate = sums / counts[:, None, None]
    seasonal = jnp.einsum("md,mlc->dlc", onehot.astype(jnp.float32), climate, precision=HIGH)
    table_hot = (
        row_index[:, None] == jnp.arange(area_table.shape[0], dtype=jnp.int32)[None, :]
    ).astype(jnp.float32)
    scale = jnp.sqrt(jnp.dot(table_hot, area_table, precision=HIGH))
    weighted = (fields.astype(jnp.float32) - seasonal) * scale[None, :, None]
    days_total = fields.shape[0] * lax.axis_size("days")
    partial_pcs = jnp.einsum("dlc,klc->dk", weighted, basis.astype(jnp.float32), precision=HIGH)
    pcs = lax.psum(partial_pcs, "space")
    eofs = basis.astype(jnp.float32)
    for step_count in range(ITERS):
        partial_cover = jnp.einsum("dk,dlc->klc", pcs, weighted, precision=HIGH) / days_total
        cover = lax.psum(partial_cover, "days")
        partial_gram = self_gram(cover)
        partial_raw = jnp.einsum("dlc,klc->dk", weighted, cover, precision=HIGH)
        gram, raw_pcs = lax.psum((partial_gram, partial_raw), "space")
        lower = jnp.linalg.cholesky(gram)
        eofs = solve_lower(lower, cover)
        pcs = lax.linalg.triangular_solve(
            lower, raw_pcs, left_side=False, lower=True, transpose_a=True
        )
    return (eofs, pcs)


def solution(mesh):
    placed = (P("days", "space", None), P("days"), P("space"), P(), P(None, "space", None))
    return jax.shard_map(
        local,
        mesh=mesh,
        in_specs=placed,
        out_specs=(P(None, "space", None), P("days", None)),
        check_vma=False,
    )
```

profile of v0, /device:TPU:0, one launch (start us, length us, event | category | flops | bytes accessed | tf_op | source)
XLA Modules:
  0.0 343.0 jit_solution(18154794807191105921)
XLA Ops:
  7.3 3.1 fusion
  10.6 11.5 %psum.64 = f32[12]{0:T(128)S(1)} all-reduce(f32[12]{0:T(128)S(1)} %convert_reduce_fusion), channel_id=1, replica_groups=mesh['days'=4,'space'=8] {'days'}, use_global_device_ids=true, to_apply=%region_2.0 | all-reduce | flops 12 | bytes 96 | tf_op jit(solution)/shard_map/psum | solution.py:27
  22.2 36.2 %all-reduce.6.cloned.1.call-done = f32[12,4,1440]{2,0,1:T(8,128)} async-done(((f32[12,4,1440]{2,0,1:T(8,128)}), f32[12,4,1440]{2,0,1:T(8,128)}) %all-reduce.6.cloned.1.call-update) | async-done | bytes 276496 | tf_op jit(solution)/shard_map/psum | solution.py:27
  58.4 3.2 subtract_multiply_fusion
  63.5 2.4 convolution_bitcast_fusion.4
  65.9 28.5 %psum.65 = f32[160,64]{0,1:T(8,128)S(1)} all-reduce(f32[160,64]{0,1:T(8,128)S(1)} %convolution_bitcast_fusion.4), channel_id=1, replica_groups=mesh['days'=4,'space'=8] {'space'}, use_global_device_ids=true, to_apply=%region_3.0 | all-reduce | flops 10240 | bytes 81920 | tf_op jit(solution)/shard_map/psum | solution.py:37
  94.4 5.4 %convolution_multiply_fusion.1 = f32[64,4,1440]{2,0,1:T(8,128)} fusion(f32[160,4,1440]{2,0,1:T(8,128)} %copy-done.1, f32[160,64]{0,1:T(8,128)S(1)} %psum.65), kind=kOutput, calls=%fused_computation.2 | convolution fusion | flops 708157440 | bytes 5201920 | tf_op jit(solution)/shard_map/dk,dlc->klc/dot_general | solution.py:40
  100.1 57.9 %all-reduce.8.cloned.1.call-done = f32[64,4,1440]{2,0,1:T(8,128)} async-done(((f32[64,4,1440]{2,0,1:T(8,128)}), f32[64,4,1440]{2,0,1:T(8,128)}) %all-reduce.8.cloned.1.call-update) | async-done | bytes 1474576 | tf_op jit(solution)/shard_map/psum | solution.py:41
  157.9 3.5 %convolution_bitcast_fusion.6 = f32[64,64]{0,1:T(8,128)S(1)} fusion(f32[64,4,1440]{2,0,1:T(8,128)} %all-reduce.8.cloned.1.call-done), kind=kOutput, calls=%fused_computation.13 | convolution fusion | flops 283115520 | bytes 1490944 | tf_op jit(solution)/shard_map/klc,jlc->kj/dot_general | solution.py:19
  161.4 5.3 %convolution_bitcast_fusion.1 = f32[160,64]{1,0:T(8,128)S(1)} fusion(f32[160,4,1440]{2,0,1:T(8,128)} %copy-done.1, f32[64,4,1440]{2,0,1:T(8,128)S(1)} %copy-done.3), kind=kOutput, calls=%fused_computation.8 | convolution fusion | flops 707788800 | bytes 5201920 | tf_op jit(solution)/shard_map/dlc,klc->dk/dot_general | solution.py:43
  166.7 29.8 %all-reduce.1 = (f32[160,64]{1,0:T(8,128)S(1)}, f32[64,64]{0,1:T(8,128)S(1)}) all-reduce(f32[160,64]{1,0:T(8,128)S(1)} %convolution_bitcast_fusion.1, f32[64,64]{0,1:T(8,128)S(1)} %convolution_bitcast_fusion.6), channel_id=1, replica_groups=mesh['days'=4,'space'=8] {'space'}, use_global_device_ids=true, to_apply=%region_8.0 | all-reduce | flops 14336 | bytes 114688 | tf_op jit(solution)/shard_map/psum | solution.py:44
  196.7 5.8 %cholesky.44 = f32[64,64]{1,0:T(8,128)S(1)} custom-call(f32[64,64]{1,0:T(8,128)S(1)} %fusion.15), custom_call_target="Cholesky" | custom-call | tf_op jit(solution)/shard_map/jit(cholesky)/cholesky | solution.py:45
  203.8 4.9 %custom-call.10 = f32[1,64,64]{1,2,0:T(8,128)S(1)} custom-call(f32[1,64,64]{2,1,0:T(8,128)S(1)} %fusion.9), custom_call_target="InvertDiagBlocksLowerTriangular" | custom-call | tf_op jit(solution)/shard_map/triangular_solve/custom-call.0 | solution.py:47
  209.1 5.4 %convolution_multiply_fusion = f32[64,4,1440]{2,0,1:T(8,128)} fusion(f32[160,64,1]{0,1,2:T(8,128)S(1)} %convolution_bitcast_fusion.3, f32[160,4,1440]{2,0,1:T(8,128)} %copy-done.1), kind=kOutput, calls=%fused_computation.1 | convolution fusion | flops 708157440 | bytes 5201920 | tf_op jit(solution)/shard_map/dk,dlc->klc/dot_general | solution.py:40
  214.5 58.1 %all-reduce.10.cloned.1.call-done = f32[64,4,1440]{2,0,1:T(8,128)} async-done(((f32[64,4,1440]{2,0,1:T(8,128)}), f32[64,4,1440]{2,0,1:T(8,128)}) %all-reduce.10.cloned.1.call-update) | async-done | bytes 1474576 | tf_op jit(solution)/shard_map/psum | solution.py:41
  272.6 3.6 %copy.19 = f32[64,4,1440]{2,1,0:T(4,128)} copy(f32[64,4,1440]{2,0,1:T(8,128)} %all-reduce.10.cloned.1.call-done) | data formatting | bytes 2949120 | tf_op jit(solution)/shard_map/psum | solution.py:41
  276.2 3.3 reshape.27
  279.5 5.3 %convolution_bitcast_fusion = f32[160,64]{1,0:T(8,128)S(1)} fusion(f32[160,4,1440]{2,0,1:T(8,128)} %copy-done.1, f32[64,4,1440]{2,0,1:T(8,128)S(1)} %copy-done.2), kind=kOutput, calls=%fused_computation.7 | convolution fusion | flops 707788800 | bytes 5201920 | tf_op jit(solution)/shard_map/dlc,klc->dk/dot_general | solution.py:43
  286.2 30.2 %all-reduce = (f32[64,64]{0,1:T(8,128)S(1)}, f32[160,64]{1,0:T(8,128)S(1)}) all-reduce(f32[64,64]{0,1:T(8,128)S(1)} %convolution_bitcast_fusion.5, f32[160,64]{1,0:T(8,128)S(1)} %convolution_bitcast_fusion), channel_id=1, replica_groups=mesh['days'=4,'space'=8] {'space'}, use_global_device_ids=true, to_apply=%region_10.13 | all-reduce | flops 14336 | bytes 114688 | tf_op jit(solution)/shard_map/psum | solution.py:44
  316.5 5.8 %cholesky.55 = f32[64,64]{1,0:T(8,128)S(1)} custom-call(f32[64,64]{1,0:T(8,128)S(1)} %fusion.13), custom_call_target="Cholesky" | custom-call | tf_op jit(solution)/shard_map/jit(cholesky)/cholesky | solution.py:45
  323.7 4.9 %custom-call.8 = f32[1,64,64]{1,2,0:T(8,128)S(1)} custom-call(f32[1,64,64]{2,1,0:T(8,128)S(1)} %fusion.10), custom_call_target="InvertDiagBlocksLowerTriangular" | custom-call | tf_op jit(solution)/shard_map/triangular_solve | solution.py:12
  328.6 2.9 triangular_solve.34
  332.5 1.9 fusion.2
  334.4 2.2 copy.22
  (37 shorter events, 8.0 us)
Async XLA Ops:
  7.2 56.3 %copy-start = (bf16[64,4,1440]{2,1,0:T(4,128)(2,1)S(1)}, bf16[64,4,1440]{2,1,0:T(4,128)(2,1)}, u32[]{:S(2)}) copy-start(bf16[64,4,1440]{2,1,0:T(4,128)(2,1)} %param.12) | copy-start | bytes 2211844
  7.2 3.3 copy-start.5
  7.2 51.2 %copy-start.4 = (bf16[160,4,1440]{2,1,0:T(4,128)(2,1)S(1)}, bf16[160,4,1440]{2,1,0:T(4,128)(2,1)}, u32[]{:S(2)}) copy-start(bf16[160,4,1440]{2,1,0:T(4,128)(2,1)} %param.8) | copy-start | bytes 5529604
  7.2 14.8 %copy-start.7 = (f32[32]{0:T(128)S(1)}, f32[32]{0:T(128)}, u32[]{:S(2)}) copy-start(f32[32]{0:T(128)} %param.11) | copy-start | bytes 388
  7.2 14.8 %copy-start.6 = (s32[4]{0:T(128)S(1)}, s32[4]{0:T(128)}, u32[]{:S(2)}) copy-start(s32[4]{0:T(128)} %param.10) | copy-start | bytes 52
  7.2 51.2 %all-reduce.6.cloned.1.call-start = ((), (), s32[]{:S(2)}) async-start(), calls=%async_computation | async-start | bytes 786432 | tf_op jit(solution)/shard_map/psum | solution.py:27
  10.4 147.5 %all-reduce.8.cloned.1.call-start = ((), (), s32[]{:S(2)}) async-start(), calls=%async_computation.1 | async-start | bytes 3145728 | tf_op jit(solution)/shard_map/psum | solution.py:41
  61.6 1.9 copy-start.1
  99.8 172.8 %all-reduce.10.cloned.1.call-start = ((), (), s32[]{:S(2)}) async-start(), calls=%async_computation.2 | async-start | bytes 3145728 | tf_op jit(solution)/shard_map/psum | solution.py:41
  157.9 3.5 %copy-start.3 = (f32[64,4,1440]{2,0,1:T(8,128)S(1)}, f32[64,4,1440]{2,0,1:T(8,128)}, u32[]{:S(2)}) copy-start(f32[64,4,1440]{2,0,1:T(8,128)} %all-reduce.8.cloned.1.call-done) | copy-start | bytes 4423684
  276.2 3.3 copy-start.2
Sparse Core Ops, SparseCore 0:
  11.6 46.8 all-reduce.5
  99.9 57.9 all-reduce.7
  214.6 57.9 all-reduce.9
where the time goes:
time: 343 us
  waiting for transfers between devices  152 us (44%)
  blocking collectives  100 us (29%)
  matrix products  38.3 us (11%)
  other arithmetic  24.3 us (7%)
  local copies, waits for them, and re-layouts  14 us (4%)
  between operations  13.9 us (4%)
    psum x2, waiting for transfers between devices, local(): cover = lax.psum(partial_cover, 'days')  116 us
    psum x2, blocking collectives, local(): gram, raw_pcs = lax.psum((partial_gram, partial_raw), 'space')  60 us
    psum x1, waiting for transfers between devices, local(): sums, counts = lax.psum((sums, counts), 'days')  36.2 us
    psum x1, blocking collectives, local(): pcs = lax.psum(partial_pcs, 'space')  28.5 us
    another operation x6, other arithmetic, local(): lower = jnp.linalg.cholesky(gram)  13 us
    psum x1, blocking collectives, local(): sums, counts = lax.psum((sums, counts), 'days')  11.5 us
    dot_general x2, matrix products, local(): jnp.einsum('dk,dlc->klc', pcs, weighted, precision=HIGH) / days_total  10.8 us
    dot_general x2, matrix products, local(): partial_raw = jnp.einsum('dlc,klc->dk', weighted, cover, precision=HIGH)  10.6 us
  transfers between devices with their start and end apart: 3, of which 3 were waited for; matrix products, arithmetic and copies ran while one was open for 0% of the time, Pallas kernels for 0%

commit v1 on v0

--- a/solution.py
+++ b/solution.py
@@ -38,7 +38,8 @@
     eofs = basis.astype(jnp.float32)
     for step_count in range(ITERS):
         partial_cover = jnp.einsum("dk,dlc->klc", pcs, weighted, precision=HIGH) / days_total
-        cover = lax.psum(partial_cover, "days")
+        current_arr = lax.all_gather(partial_cover, "days")
+        cover = jnp.sum(current_arr, 0)
         partial_gram = self_gram(cover)
         partial_raw = jnp.einsum("dlc,klc->dk", weighted, cover, precision=HIGH)
         gram, raw_pcs = lax.psum((partial_gram, partial_raw), "space")

time: 343 us -> 366 us (1.067)
  waiting for transfers between devices: 152 us -> 171 us
  other arithmetic: 24.3 us -> 31.5 us
    all_gather x0 -> x2, waiting for transfers between devices: none -> 135 us  [local(): current_arr = lax.all_gather(partial_cover, 'days')]
    psum x2 -> x0, waiting for transfers between devices: 116 us -> none  [local(): cover = lax.psum(partial_cover, 'days')]
    reduce_sum x0 -> x2, other arithmetic: none -> 7.22 us  [local(): cover = jnp.sum(current_arr, 0)]
where the time goes in v1:
time: 366 us; the launch traced here: 365 us
  waiting for transfers between devices  171 us (47%)
  blocking collectives  98.9 us (27%)
  matrix products  37.6 us (10%)
  other arithmetic  31.5 us (9%)
  between operations  13.9 us (4%)
  local copies, waits for them, and re-layouts  12.5 us (3%)
    all_gather x2, waiting for transfers between devices, local(): current_arr = lax.all_gather(partial_cover, 'days')  135 us
    psum x2, blocking collectives, local(): gram, raw_pcs = lax.psum((partial_gram, partial_raw), 'space')  58.9 us
    psum x1, waiting for transfers between devices, local(): sums, counts = lax.psum((sums, counts), 'days')  36.2 us
    psum x1, blocking collectives, local(): pcs = lax.psum(partial_pcs, 'space')  28.5 us
    another operation x6, other arithmetic, local(): lower = jnp.linalg.cholesky(gram)  13 us
    dot_general x2, matrix products, local(): partial_raw = jnp.einsum('dlc,klc->dk', weighted, cover, precision=HIGH)  12.1 us
    psum x1, blocking collectives, local(): sums, counts = lax.psum((sums, counts), 'days')  11.5 us
    dot_general x2, matrix products, local(): jnp.einsum('dk,dlc->klc', pcs, weighted, precision=HIGH) / days_total  10.8 us
  transfers between devices with their start and end apart: 3, of which 3 were waited for; matrix products, arithmetic and copies ran while one was open for 0% of the time, Pallas kernels for 0%

profile of v1, /device:TPU:0, one launch (start us, length us, event | category | flops | bytes accessed | tf_op | source)
XLA Modules:
  0.0 365.4 jit_solution(5898519945724968898)
XLA Ops:
  7.3 3.1 fusion
  10.6 11.5 %psum.50 = f32[12]{0:T(128)S(1)} all-reduce(f32[12]{0:T(128)S(1)} %convert_reduce_fusion), channel_id=1, replica_groups=mesh['days'=4,'space'=8] {'days'}, use_global_device_ids=true, to_apply=%region_2.0 | all-reduce | flops 12 | bytes 96 | tf_op jit(solution)/shard_map/psum | solution.py:27
  22.2 36.2 %all-reduce.4.cloned.1.call-done = f32[12,4,1440]{2,0,1:T(8,128)} async-done(((f32[12,4,1440]{2,0,1:T(8,128)}), f32[12,4,1440]{2,0,1:T(8,128)}) %all-reduce.4.cloned.1.call-update) | async-done | bytes 276496 | tf_op jit(solution)/shard_map/psum | solution.py:27
  58.4 3.2 subtract_multiply_fusion
  63.5 2.4 convolution_bitcast_fusion.4
  66.0 28.5 %psum.51 = f32[160,64]{0,1:T(8,128)S(1)} all-reduce(f32[160,64]{0,1:T(8,128)S(1)} %convolution_bitcast_fusion.4), channel_id=1, replica_groups=mesh['days'=4,'space'=8] {'space'}, use_global_device_ids=true, to_apply=%region_3.0 | all-reduce | flops 10240 | bytes 81920 | tf_op jit(solution)/shard_map/psum | solution.py:37
  94.5 5.4 %convolution_multiply_fusion.1 = f32[64,4,1440]{2,0,1:T(8,128)} fusion(f32[160,4,1440]{2,0,1:T(8,128)} %copy-done.1, f32[160,64]{0,1:T(8,128)S(1)} %psum.51), kind=kOutput, calls=%fused_computation.2 | convolution fusion | flops 708157440 | bytes 5201920 | tf_op jit(solution)/shard_map/dk,dlc->klc/dot_general | solution.py:40
  100.1 67.2 %all-gather.5.cloned.1.call-done = f32[256,4,1440]{2,0,1:T(8,128)} async-done(((f32[64,4,1440]{2,0,1:T(8,128)}), f32[256,4,1440]{2,0,1:T(8,128)}) %all-gather.5.cloned.1.call-update) | async-done | bytes 5898256 | tf_op jit(solution)/shard_map/all_gather | solution.py:41
  167.3 3.6 reduce_sum.28
  172.3 6.1 %convolution_bitcast_fusion.1 = f32[160,64]{0,1:T(8,128)S(1)} fusion(f32[160,4,1440]{2,0,1:T(8,128)} %copy-done.1, f32[64,4,1440]{2,0,1:T(8,128)S(1)} %reduce_sum.28), kind=kOutput, calls=%fused_computation.8 | convolution fusion | flops 707788800 | bytes 5201920 | tf_op jit(solution)/shard_map/dlc,klc->dk/dot_general | solution.py:44
  178.3 29.6 %all-reduce.1 = (f32[160,64]{0,1:T(8,128)S(1)}, f32[64,64]{0,1:T(8,128)S(1)}) all-reduce(f32[160,64]{0,1:T(8,128)S(1)} %convolution_bitcast_fusion.1, f32[64,64]{0,1:T(8,128)S(1)} %convolution_bitcast_fusion.6), channel_id=1, replica_groups=mesh['days'=4,'space'=8] {'space'}, use_global_device_ids=true, to_apply=%region_8.0 | all-reduce | flops 14336 | bytes 114688 | tf_op jit(solution)/shard_map/psum | solution.py:45
  208.0 5.8 %cholesky.44 = f32[64,64]{1,0:T(8,128)S(1)} custom-call(f32[64,64]{1,0:T(8,128)S(1)} %fusion.15), custom_call_target="Cholesky" | custom-call | tf_op jit(solution)/shard_map/jit(cholesky)/cholesky | solution.py:46
  215.2 4.9 %custom-call.10 = f32[1,64,64]{1,2,0:T(8,128)S(1)} custom-call(f32[1,64,64]{2,1,0:T(8,128)S(1)} %fusion.9), custom_call_target="InvertDiagBlocksLowerTriangular" | custom-call | tf_op jit(solution)/shard_map/triangular_solve/custom-call.0 | solution.py:48
  220.3 5.4 %convolution_multiply_fusion = f32[64,4,1440]{2,0,1:T(8,128)} fusion(f32[160,64,1]{0,1,2:T(8,128)S(1)} %convolution_bitcast_fusion.3, f32[160,4,1440]{2,0,1:T(8,128)} %copy-done.1), kind=kOutput, calls=%fused_computation.1 | convolution fusion | flops 708157440 | bytes 5201920 | tf_op jit(solution)/shard_map/dk,dlc->klc/dot_general | solution.py:40
  225.8 67.4 %all-gather.7.cloned.1.call-done = f32[256,4,1440]{2,0,1:T(8,128)} async-done(((f32[64,4,1440]{2,0,1:T(8,128)}), f32[256,4,1440]{2,0,1:T(8,128)}) %all-gather.7.cloned.1.call-update) | async-done | bytes 5898256 | tf_op jit(solution)/shard_map/all_gather | solution.py:41
  293.2 3.6 reduce_sum.29
  296.8 6.1 %convolution_bitcast_fusion = f32[160,64]{0,1:T(8,128)S(1)} fusion(f32[160,4,1440]{2,0,1:T(8,128)} %copy-done.1, f32[64,4,1440]{2,0,1:T(8,128)S(1)} %reduce_sum.29), kind=kOutput, calls=%fused_computation.7 | convolution fusion | flops 707788800 | bytes 5201920 | tf_op jit(solution)/shard_map/dlc,klc->dk/dot_general | solution.py:44
  304.2 2.2 copy.31
  306.4 3.2 reshape.27
  309.6 29.3 %all-reduce = (f32[64,64]{0,1:T(8,128)S(1)}, f32[160,64]{0,1:T(8,128)S(1)}) all-reduce(f32[64,64]{0,1:T(8,128)S(1)} %convolution_bitcast_fusion.5, f32[160,64]{0,1:T(8,128)S(1)} %convolution_bitcast_fusion), channel_id=1, replica_groups=mesh['days'=4,'space'=8] {'space'}, use_global_device_ids=true, to_apply=%region_10.13 | all-reduce | flops 14336 | bytes 114688 | tf_op jit(solution)/shard_map/psum | solution.py:45
  339.0 5.8 %cholesky.55 = f32[64,64]{1,0:T(8,128)S(1)} custom-call(f32[64,64]{1,0:T(8,128)S(1)} %fusion.13), custom_call_target="Cholesky" | custom-call | tf_op jit(solution)/shard_map/jit(cholesky)/cholesky | solution.py:46
  346.2 4.9 %custom-call.8 = f32[1,64,64]{1,2,0:T(8,128)S(1)} custom-call(f32[1,64,64]{2,1,0:T(8,128)S(1)} %fusion.10), custom_call_target="InvertDiagBlocksLowerTriangular" | custom-call | tf_op jit(solution)/shard_map/triangular_solve | solution.py:12
  351.1 2.9 triangular_solve.34
  356.8 2.2 copy.34
  (35 shorter events, 11.2 us)
Async XLA Ops:
  7.2 56.4 %copy-start = (bf16[64,4,1440]{2,1,0:T(4,128)(2,1)S(1)}, bf16[64,4,1440]{2,1,0:T(4,128)(2,1)}, u32[]{:S(2)}) copy-start(bf16[64,4,1440]{2,1,0:T(4,128)(2,1)} %param.12) | copy-start | bytes 2211844
  7.2 3.3 copy-start.3
  7.2 51.2 %copy-start.2 = (bf16[160,4,1440]{2,1,0:T(4,128)(2,1)S(1)}, bf16[160,4,1440]{2,1,0:T(4,128)(2,1)}, u32[]{:S(2)}) copy-start(bf16[160,4,1440]{2,1,0:T(4,128)(2,1)} %param.8) | copy-start | bytes 5529604
  7.2 14.8 %copy-start.5 = (f32[32]{0:T(128)S(1)}, f32[32]{0:T(128)}, u32[]{:S(2)}) copy-start(f32[32]{0:T(128)} %param.11) | copy-start | bytes 388
  7.2 14.8 %copy-start.4 = (s32[4]{0:T(128)S(1)}, s32[4]{0:T(128)}, u32[]{:S(2)}) copy-start(s32[4]{0:T(128)} %param.10) | copy-start | bytes 52
  7.2 51.2 %all-reduce.4.cloned.1.call-start = ((), (), s32[]{:S(2)}) async-start(), calls=%async_computation | async-start | bytes 786432 | tf_op jit(solution)/shard_map/psum | solution.py:27
  10.4 156.9 %all-gather.5.cloned.1.call-start = ((), (), s32[]{:S(2)}) async-start(), calls=%async_computation.1 | async-start | bytes 7864320 | tf_op jit(solution)/shard_map/all_gather | solution.py:41
  61.6 1.9 copy-start.1
  99.9 193.3 %all-gather.7.cloned.1.call-start = ((), (), s32[]{:S(2)}) async-start(), calls=%async_computation.2 | async-start | bytes 7864320 | tf_op jit(solution)/shard_map/all_gather | solution.py:41
Sparse Core Ops, SparseCore 0:
  11.6 46.8 all-reduce.3
  100.0 67.2 all-gather.4
  225.9 67.2 all-gather.6
